TPU v7x, 8 devices: a whole 2x2x1 slice. The times are simulated.
8 devices in a mesh: dp: 2 (over y, z), sp: 4 (over x, core).
Axes of the slice: x: 2, y: 2, z: 1, core: 2. Of those that a mesh axis runs over, the one named last changes fastest.
Arguments:
- q: bfloat16 [64, 96, 192], P('dp'), parts along dimension 0
- k: bfloat16 [64, 8192, 8, 192], P('dp', 'sp'), parts along dimension 0
- v: bfloat16 [64, 8192, 8, 192], P('dp', 'sp'), parts along dimension 0
Outputs:
- q: bfloat16 [64, 96, 192], P('dp'), parts along dimension 0
There are 2 independent parts. A program takes and returns all parts, laid end to end along the dimension named above; each array names one.
All inputs are finite; a program needn't handle non-finite values.
Results may differ from a plain program's by a relative error of at most 0.012.
Values are sent between devices in bfloat16 or wider.
A program may use at most 2 GiB of HBM per device.

v0:
```python
import jax
import jax.numpy as jnp
from jax import lax
from jax.sharding import PartitionSpec as P


def einsum(form, a, b):
    return jnp.einsum(form, a.astype(jnp.float32), b.astype(jnp.float32))


def part_of(q, k, v):
    grouped = q.reshape(q.shape[0], k.shape[2], -1, q.shape[2])
    scores = einsum("bgsd,bugd->bgsu", grouped, k) * q.shape[2] ** -0.5
    high = jnp.max(scores, -1, keepdims=True)
    weights = jnp.exp(scores - high)
    seen = einsum("bgsu,bugd->bgsd", weights.astype(jnp.bfloat16), v)
    return jnp.concatenate([seen, jnp.sum(weights, -1, keepdims=True), high], -1)


def together(parts):
    seen, total, high = parts[..., :-2], parts[..., -2:-1], parts[..., -1:]
    scale = jnp.exp(high - jnp.max(high, 0))
    return (jnp.sum(seen * scale, 0) / jnp.sum(total * scale, 0)).astype(jnp.bfloat16)


def solution(mesh):
    def step(q, k, v):
        return together(lax.all_gather(part_of(q, k, v), "sp")).reshape(q.shape)

    return jax.shard_map(
        step,
        mesh=mesh,
        in_specs=(P("dp", None, None), P("dp", "sp", None, None), P("dp", "sp", None, None)),
        out_specs=P("dp", None, None),
        check_vma=False,
    )
```

profile of v0, /device:TPU:0, one launch (start us, length us, event | category | flops | bytes accessed | tf_op | source)
XLA Modules:
  0.0 310.3 jit_solution(4265808459185108229)
XLA Ops:
  6.5 0.0 all-gather.3.cloned.1.call-start
  6.5 2.3 copy.38
  8.8 72.8 %multiply_reduce_fusion = (f32[32,8,12]{2,1,0:T(8,128)S(1)}, f32[32,8,12,2048]{3,2,1,0:T(8,128)}) fusion(bf16[32,2048,8,192]{1,3,2,0:T(8,128)(2,1)} %param.4, bf16[32,8,12,192]{3,0,2,1:T(8,128)(2,1)S(1)} %bitcast.17), kind=kOutput, calls=%fused_computation.1 | convolution fusion | flops 2428498944 | bytes 227684352 | tf_op jit(solution)/shard_map/bgsd,bugd->bgsu/dot_general | solution.py:8
  81.6 14.2 %fusion = f32[32,8,12]{2,1,0:T(8,128)S(1)} fusion(f32[32,8,12,2048]{3,2,1,0:T(8,128)} %get-tuple-element.11, f32[32,8,12]{2,1,0:T(8,128)S(1)} %get-tuple-element.10), kind=kLoop, calls=%fused_computation.2 | loop fusion | flops 18871296 | bytes 25190400 | tf_op jit(solution)/shard_map/reduce_sum | solution.py:17
  95.9 76.8 %fusion.2 = f32[32,8,12,192]{3,2,1,0:T(8,128)} fusion(bf16[32,2048,8,192]{1,3,2,0:T(8,128)(2,1)} %param.5, f32[32,8,12,2048]{3,2,1,0:T(8,128)} %get-tuple-element.11, f32[32,8,12]{2,1,0:T(8,128)S(1)} %get-tuple-element.10), kind=kOutput, calls=%fused_computation.4 | convolution fusion | flops 2434793472 | bytes 228864000 | tf_op jit(solution)/shard_map/bgsu,bugd->bgsd/dot_general | solution.py:8
  172.7 1.7 copy.42
  174.3 3.0 copy.43
  177.3 4.1 %pad_maximum_fusion = f32[32,8,12,194]{3,2,1,0:T(8,128)S(1)} fusion(f32[32,8,12,1]{3,2,1,0:T(8,128)} %copy.43, f32[32,8,12,1]{3,2,1,0:T(8,128)S(1)} %copy.42, f32[32,8,12,192]{3,2,1,0:T(8,128)} %fusion.2), kind=kLoop, calls=%fused_computation.9 | loop fusion | flops 1191936 | bytes 4767744 | tf_op jit(solution)/shard_map/concatenate | solution.py:17
  181.5 4.5 %copy.44 = f32[32,8,12,194]{3,1,2,0:T(8,128)} copy(f32[32,8,12,194]{3,2,1,0:T(8,128)S(1)} %pad_maximum_fusion) | data formatting | bytes 4767744 | tf_op jit(solution)/shard_map/concatenate | solution.py:17
  186.0 0.0 all-gather.3.cloned.1.call-update
  186.0 82.9 %all-gather.3.cloned.1.call-done = f32[128,8,12,194]{3,1,2,0:T(8,128)} async-done(((f32[32,8,12,194]{3,1,2,0:T(8,128)}), f32[128,8,12,194]{3,1,2,0:T(8,128)}) %all-gather.3.cloned.1.call-update) | async-done | bytes 9535504 | tf_op jit(solution)/shard_map/all_gather | solution.py:28
  269.0 12.6 %fusion.12 = (f32[4,32,8,12,1]{4,2,3,1,0:T(8,128)}, f32[32,8,12]{1,2,0:T(8,128)S(1)}, f32[4,32,8,12,1]{4,2,3,1,0:T(8,128)}) fusion(f32[4,32,8,12,194]{4,2,3,1,0:T(8,128)} %bitcast.15), kind=kLoop, calls=%fused_computation.19 | loop fusion | flops 9216 | bytes 208896 | tf_op jit(solution)/shard_map/slice | solution.py:21
  281.6 5.2 %copy.58 = f32[4,32,8,12,1]{1,2,4,3,0:T(8,128)S(1)} copy(f32[4,32,8,12,1]{4,2,3,1,0:T(8,128)} %get-tuple-element.5) | data formatting | bytes 98304
  286.8 0.1 copy.60
  286.9 5.2 %copy.57 = f32[4,32,8,12,1]{1,2,4,3,0:T(8,128)S(1)} copy(f32[4,32,8,12,1]{4,2,3,1,0:T(8,128)} %get-tuple-element.7) | data formatting | bytes 98304
  292.2 0.5 copy.46
  292.7 6.4 %fusion.6 = f32[32,8,12,192]{3,1,2,0:T(8,128)S(1)} fusion(f32[4,32,8,12,194]{4,2,3,1,0:T(8,128)} %bitcast.16, f32[4,32,8,12]{2,3,1,0:T(8,128)S(1)} %copy.46), kind=kLoop, calls=%fused_computation.8 | loop fusion | flops 4128768 | bytes 11845632 | tf_op jit(solution)/shard_map/reduce_sum | solution.py:23
  299.1 1.8 copy.48
  301.0 0.5 fusion.7
  301.4 2.0 copy.51
  (3 shorter events, 0.1 us)
Async XLA Ops:
  6.5 262.4 %all-gather.3.cloned.1.call-start = ((), (), s32[]{:S(2)}) async-start(), calls=%async_computation | async-start | bytes 15728640 | tf_op jit(solution)/shard_map/all_gather | solution.py:28
Sparse Core Ops, SparseCore 0:
  186.2 82.7 all-gather.2
where the time goes:
time: 311 us; the launch traced here: 310 us
  matrix products  150 us (48%)
  waiting for transfers between devices  83 us (27%)
  other arithmetic  37.9 us (12%)
  local copies, waits for them, and re-layouts  26.4 us (8%)
  between operations  13.5 us (4%)
    dot_general x2, matrix products, einsum(): return jnp.einsum(form, a.astype(jnp.float32), b.astype(jnp.float32))  150 us
    all_gather x1, waiting for transfers between devices, step(): return together(lax.all_gather(part_of(q, k, v), 'sp')).reshape(q.shape)  82.9 us
    reduce_sum x1, other arithmetic, part_of(): jnp.sum(weights, -1, keepdims=True)  14.2 us
    unnamed x4, local copies, waits for them, and re-layouts  12.9 us
    slice x1, other arithmetic, together(): seen, total, high = (parts[..., :-2], parts[..., -2:-1], parts[..., -1:])  12.6 us
    reduce_sum x1, other arithmetic, together(): jnp.sum(seen * scale, 0) / jnp.sum(total * scale, 0)  6.39 us
  transfers between devices with their start and end apart: 1, of which 1 were waited for; matrix products, arithmetic and copies ran while one was open for 0% of the time, Pallas kernels for 0%

commit v1 on v0

v1 whole, which is shorter than its diff:
```python
import functools

import jax
import jax.numpy as jnp
from jax import lax
from jax.experimental import pallas as pl
from jax.experimental.pallas import tpu as pltpu
from jax.sharding import PartitionSpec as P

GROUP = 4
SLOTS = 4
LAG = 3
LOG2E = 1.4426950408889634


def kernel(ranks, q_hbm, k_hbm, v_hbm, out, keys, values, queries, whole, seen, parts, stats, scales, sems, q_sem, part_send, part_recv, stat_send, stat_recv):
    me = lax.axis_index("sp")
    sequences, heads, head = q_hbm.shape
    kv_heads = k_hbm.shape[0] // sequences
    each = heads // kv_heads
    per = kv_heads // GROUP
    units = sequences * per
    factor = head**-0.5 * LOG2E
    others = [lax.rem(me + d, ranks) for d in range(1, ranks)]

    def fetch(unit, slot, source, target, row):
        return pltpu.make_async_copy(source.at[pl.ds(unit * GROUP, GROUP)], target.at[slot], sems.at[row, slot])

    def fetch_k(unit, slot):
        return fetch(unit, slot, k_hbm, keys, 0)

    def fetch_v(unit, slot):
        return fetch(unit, slot, v_hbm, values, 1)

    q_copy = pltpu.make_async_copy(q_hbm, queries, q_sem)
    q_copy.start()
    for unit in range(SLOTS):
        fetch_k(unit, unit).start()
        fetch_v(unit, unit).start()

    barrier = pltpu.get_barrier_semaphore()
    for other in others:
        pl.semaphore_signal(barrier, inc=1, device_id={"sp": other})
    pl.semaphore_wait(barrier, ranks - 1)
    whole[...] = jnp.zeros_like(whole)
    q_copy.wait()

    def send(buffer, owner, b, to, send_sem, recv_sem):
        place = buffer.at[owner, b]
        return pltpu.make_async_remote_copy(place, place, send_sem, recv_sem.at[owner, b], device_id={"sp": to})

    def sends(b):
        for d, other in enumerate(others):
            yield send(parts, me, b, other, part_send.at[d, b], part_recv)
            yield send(stats, me, b, other, stat_send.at[d, b], stat_recv)

    def attend(b):
        whole[:heads] = queries[b].astype(jnp.float32)
        lane = lax.broadcasted_iota(jnp.int32, (16, 128), 1)
        stat = jnp.zeros((16, 128), jnp.float32)
        for group in range(per):
            unit = b * per + group
            slot = lax.rem(unit, SLOTS)
            fetch_k(unit, slot).wait()
            weights = []
            for g in range(GROUP):
                row = (group * GROUP + g) * each
                query = whole[row : row + 16].astype(jnp.bfloat16)
                scores = jnp.dot(query, keys[slot, g], preferred_element_type=jnp.float32)
                high = jnp.max(scores, -1, keepdims=True)
                weight = jnp.exp2((scores - high) * factor)
                total = jnp.sum(weight, -1, keepdims=True)
                stat = jnp.where(lane == group * GROUP + g, high, stat)
                stat = jnp.where(lane == 64 + group * GROUP + g, total, stat)
                weights.append(weight.astype(jnp.bfloat16))
            fetch_v(unit, slot).wait()
            for g in range(GROUP):
                row = (group * GROUP + g) * each
                result = lax.dot_general(weights[g], values[slot, g], (((1,), (1,)), ((), ())), preferred_element_type=jnp.float32)
                seen[row : row + each] = result[:each]

            @pl.when(unit + SLOTS < units)
            def _():
                fetch_k(unit + SLOTS, slot).start()
                fetch_v(unit + SLOTS, slot).start()

        parts[me, b] = seen[...].astype(jnp.bfloat16)
        stats[me, b] = stat
        for copy in sends(b):
            copy.start()

    def together(b):
        for other in others:
            send(parts, other, b, other, part_send.at[0, b], part_recv).wait_recv()
            send(stats, other, b, other, stat_send.at[0, b], stat_recv).wait_recv()
        stat = [stats[r, b] for r in range(ranks)]
        high = functools.reduce(jnp.maximum, stat)
        scale = [jnp.exp2((s - high) * factor) for s in stat]
        total = functools.reduce(jnp.add, [pltpu.roll(s, 64, 1) * c for s, c in zip(stat, scale)])
        for r in range(ranks):
            share = scale[r] / total
            for h in range(kv_heads):
                scales[r, h * each : (h + 1) * each] = jnp.broadcast_to(share[:each, h : h + 1], (each, 128))
        result = jnp.zeros((heads, head), jnp.float32)
        for r in range(ranks):
            share = scales[r]
            share = jnp.concatenate([share, share[:, : head - 128]], -1)
            result += parts[r, b].astype(jnp.float32) * share
        out[b] = result.astype(jnp.bfloat16)

    def first(b, _):
        attend(b)
        return 0

    def later(b, _):
        attend(b)
        together(b - LAG)
        return 0

    def last(b, _):
        together(b)
        return 0

    lax.fori_loop(0, LAG, first, 0)
    lax.fori_loop(LAG, sequences, later, 0)
    lax.fori_loop(sequences - LAG, sequences, last, 0)

    def drain(b, _):
        for copy in sends(b):
            copy.wait_send()
        return 0

    lax.fori_loop(0, sequences, drain, 0)


def solution(mesh):
    ranks = mesh.shape["sp"]

    def step(q, k, v):
        sequences, tokens, kv_heads, head = k.shape
        heads = q.shape[1]
        k, v = (x.transpose(0, 2, 3, 1).reshape(sequences * kv_heads, head, tokens) for x in (k, v))
        hbm = pl.BlockSpec(memory_space=pl.ANY)
        return pl.pallas_call(
            functools.partial(kernel, ranks),
            out_shape=jax.ShapeDtypeStruct(q.shape, q.dtype),
            in_specs=[hbm, hbm, hbm],
            out_specs=pl.BlockSpec(memory_space=pltpu.VMEM),
            scratch_shapes=[
                pltpu.VMEM((SLOTS, GROUP, head, tokens), k.dtype),
                pltpu.VMEM((SLOTS, GROUP, head, tokens), v.dtype),
                pltpu.VMEM(q.shape, q.dtype),
                pltpu.VMEM((heads + 8, head), jnp.float32),
                pltpu.VMEM((heads, head), jnp.float32),
                pltpu.VMEM((ranks, sequences, heads, head), jnp.bfloat16),
                pltpu.VMEM((ranks, sequences, 16, 128), jnp.float32),
                pltpu.VMEM((ranks, heads, 128), jnp.float32),
                pltpu.SemaphoreType.DMA((2, SLOTS)),
                pltpu.SemaphoreType.DMA,
                pltpu.SemaphoreType.DMA((ranks - 1, sequences)),
                pltpu.SemaphoreType.DMA((ranks, sequences)),
                pltpu.SemaphoreType.DMA((ranks - 1, sequences)),
                pltpu.SemaphoreType.DMA((ranks, sequences)),
            ],
            compiler_params=pltpu.CompilerParams(collective_id=0, has_side_effects=True, vmem_limit_bytes=42 * 2**20),
        )(q, k, v)

    return jax.shard_map(
        step,
        mesh=mesh,
        in_specs=(P("dp", None, None), P("dp", "sp", None, None), P("dp", "sp", None, None)),
        out_specs=P("dp", None, None),
        check_vma=False,
    )
```

time: 311 us -> 131 us (0.42)
  matrix products: 150 us -> 0 us
  Pallas kernels: 0 us -> 128 us
  waiting for transfers between devices: 83 us -> 0 us
  other arithmetic: 37.9 us -> 0 us
  local copies, waits for them, and re-layouts: 26.4 us -> 2.55 us
  between operations: 13.5 us -> 0.01 us
    dot_general x2 -> x0, matrix products: 150 us -> none  [einsum(): return jnp.einsum(form, a.astype(jnp.float32), b.astype(jnp.float32))]
    pallas_call x0 -> x1, Pallas kernels: none -> 128 us  [step(): pl.pallas_call(functools.partial(kernel, ranks), out_shape=jax.ShapeDtype...]
    all_gather x1 -> x0, waiting for transfers between devices: 82.9 us -> none  [step(): return together(lax.all_gather(part_of(q, k, v), 'sp')).reshape(q.shape)]
    reduce_sum x3 -> x0, other arithmetic: 20.7 us -> none  [the longest x1 14.2 us: part_of(): jnp.sum(weights, -1, keepdims=True)]
    slice x1 -> x0, other arithmetic: 12.6 us -> none  [together(): seen, total, high = (parts[..., :-2], parts[..., -2:-1], parts[..., -1:])]
    unnamed x4 -> x3, local copies, waits for them, and re-layouts: 12.9 us -> 2.55 us
    broadcast_in_dim x2 -> x0, local copies, waits for them, and re-layouts: 4.67 us -> none  [the longest x1 3.01 us: part_of(): high = jnp.max(scores, -1, keepdims=True)]
    concatenate x1 -> x0, local copies, waits for them, and re-layouts: 4.52 us -> none  [part_of(): jnp.concatenate([seen, jnp.sum(weights, -1, keepdims=True), high], -1)]
  transfers between devices with their start and end apart: 1 -> 0, of which waited for: 1 -> 0; matrix products, arithmetic and copies ran while one was open for 0% -> 0% of each run, Pallas kernels for 0% -> 0%
where the time goes in v1:
time: 131 us
  Pallas kernels  128 us (98%)
  local copies, waits for them, and re-layouts  2.55 us (2%)
    pallas_call x1, Pallas kernels, step(): pl.pallas_call(functools.partial(kernel, ranks), out_shape=jax.ShapeDtype...  128 us

profile of v1, /device:TPU:0, one launch (start us, length us, event | category | flops | bytes accessed | tf_op | source)
XLA Modules:
  0.0 130.8 jit_solution(15253757130576120090)
XLA Ops:
  0.0 0.0 copy-start
  0.0 1.4 %copy-done = bf16[32,96,192]{2,1,0:T(8,128)(2,1)S(1)} copy-done((bf16[32,96,192]{2,1,0:T(8,128)(2,1)S(1)}, bf16[32,96,192]{2,1,0:T(8,128)(2,1)}, u32[]{:S(2)}) %copy-start) | copy-done | bytes 1179672
  1.4 128.2 %shard_map.37 = bf16[32,96,192]{2,1,0:T(8,128)(2,1)S(1)} custom-call(bf16[32,96,192]{2,1,0:T(8,128)(2,1)S(1)} %copy-done, bf16[256,192,2048]{2,1,0:T(8,128)(2,1)} %bitcast.1.k_hbm, bf16[256,192,2048]{2,1,0:T(8,128)(2,1)} %bitcast.3.v_hbm), custom_call_target="tpu_custom_call" | custom-call | tf_op jit(solution)/shard_map/pallas_call | solution.py:144
  129.6 1.1 copy.5
Async XLA Ops:
  0.0 1.4 %copy-start = (bf16[32,96,192]{2,1,0:T(8,128)(2,1)S(1)}, bf16[32,96,192]{2,1,0:T(8,128)(2,1)}, u32[]{:S(2)}) copy-start(bf16[32,96,192]{2,1,0:T(8,128)(2,1)} %q_hbm.1) | copy-start | bytes 3538948

commit v2 on v0

v2 whole, which is shorter than its diff:
```python
import functools

import jax
import jax.numpy as jnp
from jax import lax
from jax.experimental import pallas as pl
from jax.experimental.pallas import tpu as pltpu
from jax.sharding import PartitionSpec as P

GROUP = 4
SLOTS = 4
LAG = 3
PIECE = 16
LOG2E = 1.4426950408889634


def kernel(
    ranks, q_hbm, k_hbm, v_hbm, out, keys, values, queries, whole, weights, marks, seen, parts, stats, scales, k_sem, v_sem, q_sem, tail_sem, part_send, part_recv, stat_send, stat_recv, piece_send, piece_recv
):
    me = lax.axis_index("sp")
    sequences, heads, head = q_hbm.shape
    kv_heads = k_hbm.shape[0] // sequences
    each = heads // kv_heads
    per = kv_heads // GROUP
    rows = GROUP * each
    units = sequences * per
    factor = head**-0.5 * LOG2E
    others = [lax.rem(me + d, ranks) for d in (2, 1, 3)]
    final = sequences - 1

    def fetch(hbm, buffer, sem, unit):
        slot = lax.rem(unit, SLOTS)
        return pltpu.make_async_copy(hbm.at[pl.ds(unit * GROUP, GROUP)], buffer.at[slot], sem.at[slot])

    fetch_k = functools.partial(fetch, k_hbm, keys, k_sem)
    fetch_v = functools.partial(fetch, v_hbm, values, v_sem)

    def fetch_tail(g):
        return pltpu.make_async_copy(v_hbm.at[(units - 1) * GROUP + g], values.at[(units - 1) % SLOTS, g], tail_sem.at[g])

    q_copy = pltpu.make_async_copy(q_hbm, queries, q_sem)
    q_copy.start()
    for unit in range(SLOTS):
        fetch_k(unit).start()
        fetch_v(unit).start()

    barrier = pltpu.get_barrier_semaphore()
    for other in others:
        pl.semaphore_signal(barrier, inc=1, device_id={"sp": other})
    whole[...] = jnp.zeros_like(whole)
    q_copy.wait()

    def send(buffer, owner, b, to, send_sem, recv_sem):
        place = buffer.at[owner, b]
        return pltpu.make_async_remote_copy(place, place, send_sem, recv_sem.at[owner, b], device_id={"sp": to})

    def send_part(owner, b, d):
        return send(parts, owner, b, others[d], part_send.at[d, b], part_recv)

    def send_stat(owner, b, d):
        return send(stats, owner, b, others[d], stat_send.at[d, b], stat_recv)

    def send_piece(owner, n, d):
        first, size = (0, rows) if n == 0 else (rows + (n - 1) * PIECE, PIECE)
        place = parts.at[owner, final, pl.ds(first, size)]
        return pltpu.make_async_remote_copy(place, place, piece_send.at[d, n], piece_recv.at[owner, n], device_id={"sp": others[d]})

    pieces = 1 + (heads - rows) // PIECE
    lane = lax.broadcasted_iota(jnp.int32, (16, 128), 1)

    def load_queries(b):
        whole[:heads] = queries[b].astype(jnp.float32)

    def weigh(slot, part):
        mark = jnp.zeros((16, 128), jnp.float32) if part == 0 else marks[...]
        for g in range(GROUP):
            h = part * GROUP + g
            query = whole[h * each : h * each + 16].astype(jnp.bfloat16)
            scores = jnp.dot(query, keys[slot, g], preferred_element_type=jnp.float32)
            high = jnp.max(scores, -1, keepdims=True)
            weight = jnp.exp2((scores - high) * factor)
            total = jnp.sum(weight, -1, keepdims=True)
            mark = jnp.where(lane == h, high, mark)
            mark = jnp.where(lane == 64 + h, total, mark)
            weights[part, g] = weight.astype(jnp.bfloat16)
        marks[...] = mark

    def weighted(slot, part, g, first, size):
        a, b = weights[part, g, :, first : first + size], values[slot, g, :, first : first + size]
        return lax.dot_general(a, b, (((1,), (1,)), ((), ())), preferred_element_type=jnp.float32)

    def keep(part, g, result):
        row = (part * GROUP + g) * each
        seen[row : row + each] = result[:each]

    def gather(slot, part, g):
        keep(part, g, weighted(slot, part, g, 0, values.shape[-1]))

    def pack(b, first, size):
        parts[me, b, first : first + size] = seen[first : first + size].astype(jnp.bfloat16)

    def shares(b):
        stat = [stats[r, b] for r in range(ranks)]
        high = functools.reduce(jnp.maximum, stat)
        scale = [jnp.exp2((s - high) * factor) for s in stat]
        total = functools.reduce(jnp.add, [pltpu.roll(s, 64, 1) * c for s, c in zip(stat, scale)])
        for r in range(ranks):
            share = scale[r] / total
            for h in range(kv_heads):
                scales[r, h * each : (h + 1) * each] = jnp.broadcast_to(share[:each, h : h + 1], (each, 128))

    def combine(b, first, size):
        place = slice(first, first + size)
        result = jnp.zeros((size, head), jnp.float32)
        for r in range(ranks):
            share = scales[r, place]
            share = jnp.concatenate([share, share[:, : head - 128]], -1)
            result += parts[r, b, place].astype(jnp.float32) * share
        out[b, place] = result.astype(jnp.bfloat16)

    def arrive(b):
        for d, other in enumerate(others):
            send_part(me, b, d).wait_send()
            send_stat(me, b, d).wait_send()
            send_part(other, b, d).wait_recv()
            send_stat(other, b, d).wait_recv()

    def together(b):
        shares(b)
        combine(b, 0, heads)

    def start(copy, unit):
        @pl.when(unit < units)
        def _():
            copy(unit).start()

    def start_v(unit):
        @pl.when(unit < units - 1)
        def _():
            fetch_v(unit).start()

        @pl.when(unit == units - 1)
        def _():
            for g in range(GROUP):
                fetch_tail(g).start()

    def turn(b, part, lag):
        unit = b * per + part
        after = (part + 1) % per
        fetch_k(unit + 1).wait()
        fetch_v(unit).wait()
        if part == 0 and lag:
            arrive(b - lag)
        if after == 0:
            load_queries(b + 1)
        weigh(lax.rem(unit + 1, SLOTS), after)
        slot = lax.rem(unit, SLOTS)
        for g in range(GROUP):
            gather(slot, part, g)
        if part == 0 and lag:
            together(b - lag)
        start(fetch_k, unit + 1 + SLOTS)
        start_v(unit + SLOTS)

    def attend(b, lag):
        turn(b, 0, lag)
        stats[me, b] = marks[...]
        turn(b, 1, 0)
        pack(b, 0, heads)
        for d in range(ranks - 1):
            send_part(me, b, d).start()
            send_stat(me, b, d).start()

    load_queries(0)
    fetch_k(0).wait()
    weigh(0, 0)
    start(fetch_k, SLOTS)
    pl.semaphore_wait(barrier, ranks - 1)

    def early(b, _):
        attend(b, 0)
        return 0

    def later(b, _):
        attend(b, LAG)
        return 0

    lax.fori_loop(0, LAG, early, 0)
    lax.fori_loop(LAG, final, later, 0)

    turn(final, 0, LAG)
    stats[me, final] = marks[...]
    pack(final, 0, rows)
    for d in range(ranks - 1):
        send_stat(me, final, d).start()
        send_piece(me, 0, d).start()
    sent = 1
    half = values.shape[-1] // 2
    waiting = None
    for g in range(GROUP + 1):
        if g < GROUP:
            fetch_tail(g).wait()
            result = sum(weighted((units - 1) % SLOTS, 1, g, first, half) for first in (0, half))
        if g > 0:
            keep(1, g - 1, waiting)
        waiting = result
        while sent < pieces and rows + sent * PIECE <= rows + g * each:
            pack(final, rows + (sent - 1) * PIECE, PIECE)
            for d in range(ranks - 1):
                send_piece(me, sent, d).start()
            sent += 1
    for b in range(final - LAG + 1, final):
        arrive(b)
        together(b)
    for d, other in enumerate(others):
        send_stat(me, final, d).wait_send()
        send_stat(other, final, d).wait_recv()
    shares(final)
    for n in range(pieces):
        for d, other in enumerate(others):
            send_piece(other, n, d).wait_recv()
        if n == 0:
            combine(final, 0, rows)
        else:
            combine(final, rows + (n - 1) * PIECE, PIECE)
    for n in range(pieces):
        for d in range(ranks - 1):
            send_piece(me, n, d).wait_send()


def solution(mesh):
    ranks = mesh.shape["sp"]

    def step(q, k, v):
        sequences, tokens, kv_heads, head = k.shape
        heads = q.shape[1]
        k, v = (x.transpose(0, 2, 3, 1).reshape(sequences * kv_heads, head, tokens) for x in (k, v))
        hbm = pl.BlockSpec(memory_space=pltpu.HBM)
        dma = pltpu.SemaphoreType.DMA
        pieces = 1 + (heads - GROUP * heads // kv_heads) // PIECE
        return pl.pallas_call(
            functools.partial(kernel, ranks),
            out_shape=jax.ShapeDtypeStruct(q.shape, q.dtype),
            in_specs=[hbm, hbm, hbm],
            out_specs=pl.BlockSpec(memory_space=pltpu.VMEM),
            scratch_shapes=[
                pltpu.VMEM((SLOTS, GROUP, head, tokens), k.dtype),
                pltpu.VMEM((SLOTS, GROUP, head, tokens), v.dtype),
                pltpu.VMEM(q.shape, q.dtype),
                pltpu.VMEM((heads + 8, head), jnp.float32),
                pltpu.VMEM((2, GROUP, 16, tokens), jnp.bfloat16),
                pltpu.VMEM((16, 128), jnp.float32),
                pltpu.VMEM((heads, head), jnp.float32),
                pltpu.VMEM((ranks, sequences, heads, head), jnp.bfloat16),
                pltpu.VMEM((ranks, sequences, 16, 128), jnp.float32),
                pltpu.VMEM((ranks, heads, 128), jnp.float32),
                dma((SLOTS,)),
                dma((SLOTS,)),
                dma,
                dma((GROUP,)),
                dma((ranks - 1, sequences)),
                dma((ranks, sequences)),
                dma((ranks - 1, sequences)),
                dma((ranks, sequences)),
                dma((ranks - 1, pieces)),
                dma((ranks, pieces)),
            ],
            compiler_params=pltpu.CompilerParams(collective_id=0, has_side_effects=True, vmem_limit_bytes=42 * 2**20),
        )(pltpu.with_memory_space_constraint(q, pltpu.HBM), k, v)

    return jax.shard_map(
        step,
        mesh=mesh,
        in_specs=(P("dp", None, None), P("dp", "sp", None, None), P("dp", "sp", None, None)),
        out_specs=P("dp", None, None),
        check_vma=False,
    )
```

time: 311 us -> 130 us (0.42)
  matrix products: 150 us -> 0 us
  Pallas kernels: 0 us -> 129 us
  waiting for transfers between devices: 83 us -> 0 us
  other arithmetic: 37.9 us -> 0 us
  local copies, waits for them, and re-layouts: 26.4 us -> 1.15 us
  between operations: 13.5 us -> 0.01 us
    dot_general x2 -> x0, matrix products: 150 us -> none  [einsum(): return jnp.einsum(form, a.astype(jnp.float32), b.astype(jnp.float32))]
    pallas_call x0 -> x1, Pallas kernels: none -> 129 us  [step(): pl.pallas_call(functools.partial(kernel, ranks), out_shape=jax.ShapeDtype...]
    all_gather x1 -> x0, waiting for transfers between devices: 82.9 us -> none  [step(): return together(lax.all_gather(part_of(q, k, v), 'sp')).reshape(q.shape)]
    reduce_sum x3 -> x0, other arithmetic: 20.7 us -> none  [the longest x1 14.2 us: part_of(): jnp.sum(weights, -1, keepdims=True)]
    slice x1 -> x0, other arithmetic: 12.6 us -> none  [together(): seen, total, high = (parts[..., :-2], parts[..., -2:-1], parts[..., -1:])]
    unnamed x4 -> x1, local copies, waits for them, and re-layouts: 12.9 us -> 1.15 us
    broadcast_in_dim x2 -> x0, local copies, waits for them, and re-layouts: 4.67 us -> none  [the longest x1 3.01 us: part_of(): high = jnp.max(scores, -1, keepdims=True)]
    concatenate x1 -> x0, local copies, waits for them, and re-layouts: 4.52 us -> none  [part_of(): jnp.concatenate([seen, jnp.sum(weights, -1, keepdims=True), high], -1)]
  transfers between devices with their start and end apart: 1 -> 0, of which waited for: 1 -> 0; matrix products, arithmetic and copies ran while one was open for 0% -> 0% of each run, Pallas kernels for 0% -> 0%
where the time goes in v2:
time: 130 us
  Pallas kernels  129 us (99%)
    pallas_call x1, Pallas kernels, step(): pl.pallas_call(functools.partial(kernel, ranks), out_shape=jax.ShapeDtype...  129 us

profile of v2, /device:TPU:0, one launch (start us, length us, event | category | flops | bytes accessed | tf_op | source)
XLA Modules:
  0.0 130.4 jit_solution(18125924049829353268)
XLA Ops:
  0.0 129.2 %shard_map.37 = bf16[32,96,192]{2,1,0:T(8,128)(2,1)S(1)} custom-call(bf16[32,96,192]{2,1,0:T(8,128)(2,1)} %q_hbm.1, bf16[256,192,2048]{2,1,0:T(8,128)(2,1)} %bitcast.1.k_hbm, bf16[256,192,2048]{2,1,0:T(8,128)(2,1)} %bitcast.3.v_hbm), custom_call_target="tpu_custom_call" | custom-call | tf_op jit(solution)/shard_map/pallas_call | solution.py:241
  129.2 1.1 copy.5

commit v3 on v2

--- a/solution.py
+++ b/solution.py
@@ -9,13 +9,14 @@
 
 GROUP = 4
 SLOTS = 4
-LAG = 3
+LAG = 2
+RING = 2 * LAG
 PIECE = 16
 LOG2E = 1.4426950408889634
 
 
 def kernel(
-    ranks, q_hbm, k_hbm, v_hbm, out, keys, values, queries, whole, weights, marks, seen, parts, stats, scales, k_sem, v_sem, q_sem, tail_sem, part_send, part_recv, stat_send, stat_recv, piece_send, piece_recv
+    ranks, q_hbm, k_hbm, v_hbm, out, keys, values, queries, whole, weights, marks, seen, parts, stats, scales, k_sem, v_sem, q_sem, tail_sem, part_send, part_recv, stat_send, stat_recv, piece_recv
 ):
     me = lax.axis_index("sp")
     sequences, heads, head = q_hbm.shape
@@ -50,20 +51,23 @@
     whole[...] = jnp.zeros_like(whole)
     q_copy.wait()
 
-    def send(buffer, owner, b, to, send_sem, recv_sem):
-        place = buffer.at[owner, b]
-        return pltpu.make_async_remote_copy(place, place, send_sem, recv_sem.at[owner, b], device_id={"sp": to})
+    def send(buffer, owner, b, d, send_sem, recv_sem):
+        place, turn = buffer.at[owner, b], lax.rem(b, RING)
+        return pltpu.make_async_remote_copy(place, place, send_sem, recv_sem.at[turn], device_id={"sp": others[d]})
 
     def send_part(owner, b, d):
-        return send(parts, owner, b, others[d], part_send.at[d, b], part_recv)
+        return send(parts, owner, b, d, part_send, part_recv)
 
     def send_stat(owner, b, d):
-        return send(stats, owner, b, others[d], stat_send.at[d, b], stat_recv)
+        return send(stats, owner, b, d, stat_send, stat_recv)
+
+    def piece_rows(n):
+        return (0, rows) if n == 0 else (rows + (n - 1) * PIECE, PIECE)
 
     def send_piece(owner, n, d):
-        first, size = (0, rows) if n == 0 else (rows + (n - 1) * PIECE, PIECE)
+        first, size = piece_rows(n)
         place = parts.at[owner, final, pl.ds(first, size)]
-        return pltpu.make_async_remote_copy(place, place, piece_send.at[d, n], piece_recv.at[owner, n], device_id={"sp": others[d]})
+        return pltpu.make_async_remote_copy(place, place, part_send, piece_recv.at[n], device_id={"sp": others[d]})
 
     pieces = 1 + (heads - rows) // PIECE
     lane = lax.broadcasted_iota(jnp.int32, (16, 128), 1)
@@ -118,12 +122,13 @@
             result += parts[r, b, place].astype(jnp.float32) * share
         out[b, place] = result.astype(jnp.bfloat16)
 
-    def arrive(b):
-        for d, other in enumerate(others):
-            send_part(me, b, d).wait_send()
-            send_stat(me, b, d).wait_send()
-            send_part(other, b, d).wait_recv()
-            send_stat(other, b, d).wait_recv()
+    def arrive(buffer, sem, *place):
+        theirs = buffer.at[(pl.ds(0, ranks - 1), *place)]
+        pltpu.make_async_copy(theirs, theirs, sem).wait()
+
+    def arrive_all(b):
+        arrive(parts, part_recv.at[lax.rem(b, RING)], b)
+        arrive(stats, stat_recv.at[lax.rem(b, RING)], b)
 
     def together(b):
         shares(b)
@@ -149,23 +154,23 @@
         after = (part + 1) % per
         fetch_k(unit + 1).wait()
         fetch_v(unit).wait()
-        if part == 0 and lag:
-            arrive(b - lag)
+        if lag:
+            arrive_all(b - lag)
         if after == 0:
             load_queries(b + 1)
         weigh(lax.rem(unit + 1, SLOTS), after)
         slot = lax.rem(unit, SLOTS)
         for g in range(GROUP):
             gather(slot, part, g)
-        if part == 0 and lag:
+        if lag:
             together(b - lag)
         start(fetch_k, unit + 1 + SLOTS)
         start_v(unit + SLOTS)
 
     def attend(b, lag):
-        turn(b, 0, lag)
+        turn(b, 0, 0)
         stats[me, b] = marks[...]
-        turn(b, 1, 0)
+        turn(b, 1, lag)
         pack(b, 0, heads)
         for d in range(ranks - 1):
             send_part(me, b, d).start()
@@ -210,22 +215,16 @@
                 send_piece(me, sent, d).start()
             sent += 1
     for b in range(final - LAG + 1, final):
-        arrive(b)
+        arrive_all(b)
         together(b)
-    for d, other in enumerate(others):
-        send_stat(me, final, d).wait_send()
-        send_stat(other, final, d).wait_recv()
+    arrive(stats, stat_recv.at[final % RING], final)
     shares(final)
     for n in range(pieces):
-        for d, other in enumerate(others):
-            send_piece(other, n, d).wait_recv()
-        if n == 0:
-            combine(final, 0, rows)
-        else:
-            combine(final, rows + (n - 1) * PIECE, PIECE)
-    for n in range(pieces):
-        for d in range(ranks - 1):
-            send_piece(me, n, d).wait_send()
+        first, size = piece_rows(n)
+        arrive(parts, piece_recv.at[n], final, pl.ds(first, size))
+        combine(final, first, size)
+    arrive(parts, part_send)
+    arrive(stats, stat_send)
 
 
 def solution(mesh):
@@ -258,12 +257,11 @@
                 dma((SLOTS,)),
                 dma,
                 dma((GROUP,)),
-                dma((ranks - 1, sequences)),
-                dma((ranks, sequences)),
-                dma((ranks - 1, sequences)),
-                dma((ranks, sequences)),
-                dma((ranks - 1, pieces)),
-                dma((ranks, pieces)),
+                dma,
+                dma((RING,)),
+                dma,
+                dma((RING,)),
+                dma((pieces,)),
             ],
             compiler_params=pltpu.CompilerParams(collective_id=0, has_side_effects=True, vmem_limit_bytes=42 * 2**20),
         )(pltpu.with_memory_space_constraint(q, pltpu.HBM), k, v)

time: 130 us -> 126 us (0.969)
  Pallas kernels: 129 us -> 125 us
    pallas_call x1, Pallas kernels: 129 us -> 125 us  [step(): pl.pallas_call(functools.partial(kernel, ranks), out_shape=jax.ShapeDtype...]
where the time goes in v3:
time: 126 us
  Pallas kernels  125 us (99%)
    pallas_call x1, Pallas kernels, step(): pl.pallas_call(functools.partial(kernel, ranks), out_shape=jax.ShapeDtype...  125 us

profile of v3, /device:TPU:0, one launch (start us, length us, event | category | flops | bytes accessed | tf_op | source)
XLA Modules:
  0.0 126.2 jit_solution(5388843718902484052)
XLA Ops:
  0.0 125.0 %shard_map.37 = bf16[32,96,192]{2,1,0:T(8,128)(2,1)S(1)} custom-call(bf16[32,96,192]{2,1,0:T(8,128)(2,1)} %q_hbm.1, bf16[256,192,2048]{2,1,0:T(8,128)(2,1)} %bitcast.1.k_hbm, bf16[256,192,2048]{2,1,0:T(8,128)(2,1)} %bitcast.3.v_hbm), custom_call_target="tpu_custom_call" | custom-call | tf_op jit(solution)/shard_map/pallas_call | solution.py:240
  125.1 1.1 copy.5

commit v4 on v3

v4 whole, which is shorter than its diff:
```python
import functools

import jax
import jax.numpy as jnp
from jax import lax
from jax.experimental import pallas as pl
from jax.experimental.pallas import tpu as pltpu
from jax.sharding import PartitionSpec as P

GROUP = 4
SLOTS = 4
LAG = 2
RING = 2 * LAG + 1
PIECE = 32
PACKED = PIECE * 3 // 2
LOG2E = 1.4426950408889634


def kernel(
    ranks, q_hbm, k_hbm, v_hbm, out, keys, values, queries, whole, weights, marks, seen, parts, stats, scales, k_sem, v_sem, q_sem, tail_sem, part_send, part_recv, stat_send, stat_recv, piece_recv
):
    me = lax.axis_index("sp")
    sequences, heads, head = q_hbm.shape
    kv_heads = k_hbm.shape[0] // sequences
    each = heads // kv_heads
    per = kv_heads // GROUP
    half = GROUP // 2
    pieces = heads // PIECE
    units = sequences * per
    factor = head**-0.5 * LOG2E
    others = [lax.rem(me + d, ranks) for d in (2, 1, 3)]
    final = sequences - 1

    def fetch(hbm, buffer, sem, unit):
        slot = lax.rem(unit, SLOTS)
        return pltpu.make_async_copy(hbm.at[pl.ds(unit * GROUP, GROUP)], buffer.at[slot], sem.at[slot])

    fetch_k = functools.partial(fetch, k_hbm, keys, k_sem)
    fetch_v = functools.partial(fetch, v_hbm, values, v_sem)

    def fetch_tail(n):
        unit, first = (units - per) + n // 2, n % 2 * half
        return pltpu.make_async_copy(v_hbm.at[pl.ds(unit * GROUP + first, half)], values.at[unit % SLOTS, pl.ds(first, half)], tail_sem.at[n])

    q_copy = pltpu.make_async_copy(q_hbm, queries, q_sem)
    q_copy.start()
    fetch_k(0).start()

    def fill(unit, _):
        fetch_v(unit - 1).start()
        fetch_k(unit).start()
        return 0

    lax.fori_loop(1, SLOTS, fill, 0)
    fetch_v(SLOTS - 1).start()

    barrier = pltpu.get_barrier_semaphore()
    for other in others:
        pl.semaphore_signal(barrier, inc=1, device_id={"sp": other})
    whole[...] = jnp.zeros_like(whole)
    q_copy.wait()

    def send(place, send_sem, recv_sem):
        for other in others:
            pltpu.make_async_remote_copy(place, place, send_sem, recv_sem, device_id={"sp": other}).start()

    def send_stat(b):
        send(stats.at[me, b], stat_send, stat_recv.at[lax.rem(b, RING)])

    def send_part(b, first, size, recv_sem):
        for p in range(first, first + size):
            pack(b, p)
        send(parts.at[me, b, pl.ds(first * PACKED, size * PACKED)], part_send, recv_sem)

    lane = lax.broadcasted_iota(jnp.int32, (8, 128), 1)
    lane16 = lax.broadcasted_iota(jnp.int32, (PIECE // 2, 128), 1)

    def load_queries(b):
        whole[:heads] = queries[b].astype(jnp.float32)

    def weigh(slot, part, between):
        scores = []
        for g in range(GROUP):
            row = (part * GROUP + g) * each
            query = whole[row : row + 16].astype(jnp.bfloat16)
            scores.append(jnp.dot(query, keys[slot, g], preferred_element_type=jnp.float32))
        between()
        mark = jnp.zeros((8, 128), jnp.float32) if part == 0 else marks[...]
        for g in range(GROUP):
            h = part * GROUP + g
            high = jnp.max(scores[g], -1, keepdims=True)
            weight = jnp.exp2((scores[g] - high) * factor)
            total = jnp.sum(weight, -1, keepdims=True)
            for at, value in ((h, high), (64 + h, total)):
                mark = jnp.where(lane == at, value[:8], mark)
                mark = jnp.where(lane == at + 8, value[8:], mark)
            weights[part, g] = weight.astype(jnp.bfloat16)
        marks[...] = mark

    def gather(slot, part, g):
        row = (part * GROUP + g) * each
        result = lax.dot_general(weights[part, g], values[slot, g], (((1,), (1,)), ((), ())), preferred_element_type=jnp.float32)
        seen[row : row + each] = result[:each]

    def pack(b, p):
        rows = seen[p * PIECE : (p + 1) * PIECE]
        rest = jnp.concatenate([rows[: PIECE // 2, 128:], rows[PIECE // 2 :, 128:]], -1)
        parts[me, b, p * PACKED : p * PACKED + PIECE] = rows[:, :128].astype(jnp.bfloat16)
        parts[me, b, p * PACKED + PIECE : (p + 1) * PACKED] = rest.astype(jnp.bfloat16)

    def shares(b):
        stat = [stats[r, b] for r in range(ranks)]
        high = functools.reduce(jnp.maximum, stat)
        scale = [jnp.exp2((s - high) * factor) for s in stat]
        total = functools.reduce(jnp.add, [pltpu.roll(s, 64, 1) * c for s, c in zip(stat, scale)])
        for r in range(ranks):
            share = scale[r] / total
            for h in range(kv_heads):
                row = h * each
                scales[r, row : row + 8] = jnp.broadcast_to(share[:, h : h + 1], (8, 128))
                scales[r, row + 8 : row + each] = jnp.broadcast_to(share[: each - 8, h + 8 : h + 9], (each - 8, 128))

    def combine(b, p):
        left = right = None
        for r in range(ranks):
            share = scales[r, p * PIECE : (p + 1) * PIECE]
            both = jnp.where(lane16 < 64, share[: PIECE // 2], share[PIECE // 2 :])
            one = parts[r, b, p * PACKED : p * PACKED + PIECE].astype(jnp.float32) * share
            two = parts[r, b, p * PACKED + PIECE : (p + 1) * PACKED].astype(jnp.float32) * both
            left, right = (one, two) if r == 0 else (left + one, right + two)
        row = p * PIECE
        out[b, row : row + PIECE, :128] = left.astype(jnp.bfloat16)
        right = right.astype(jnp.bfloat16)
        out[b, row : row + PIECE // 2, 128:] = right[:, :64]
        out[b, row + PIECE // 2 : row + PIECE, 128:] = right[:, 64:]

    def arrive(buffer, sem, *place):
        theirs = buffer.at[(pl.ds(0, ranks - 1), *place)]
        pltpu.make_async_copy(theirs, theirs, sem).wait()

    def arrive_all(b):
        arrive(parts, part_recv.at[lax.rem(b, RING)], b)
        arrive(stats, stat_recv.at[lax.rem(b, RING)], b)

    def together(b):
        shares(b)
        for p in range(pieces):
            combine(b, p)

    def start(copy, unit):
        @pl.when(unit < units)
        def _():
            copy(unit).start()

    def start_v(unit):
        @pl.when(unit < units - per)
        def _():
            fetch_v(unit).start()

        for part in range(per):

            @pl.when(unit == units - per + part)
            def _():
                for n in (0, 1):
                    fetch_tail(2 * part + n).start()

    def turn(b, part, lag):
        unit = b * per + part
        after = (part + 1) % per
        fetch_k(unit + 1).wait()
        if after == 0:
            load_queries(b + 1)

        def between():
            fetch_v(unit).wait()
            if lag:
                arrive_all(b - lag)

        weigh(lax.rem(unit + 1, SLOTS), after, between)
        slot = lax.rem(unit, SLOTS)
        for g in range(GROUP):
            gather(slot, part, g)
        if lag:
            together(b - lag)
        start(fetch_k, unit + 1 + SLOTS)
        start_v(unit + SLOTS)

    def attend(b, lag):
        recv = part_recv.at[lax.rem(b, RING)]
        turn(b, 0, 0)
        stats[me, b] = marks[...]
        send_stat(b)
        send_part(b, 0, 1, recv)
        turn(b, 1, lag)
        send_part(b, 1, pieces - 1, recv)

    load_queries(0)
    fetch_k(0).wait()
    weigh(0, 0, lambda: None)
    start(fetch_k, SLOTS)
    pl.semaphore_wait(barrier, ranks - 1)

    def early(b, _):
        attend(b, 0)
        return 0

    def later(b, _):
        attend(b, LAG)
        return 0

    lax.fori_loop(0, LAG, early, 0)
    lax.fori_loop(LAG, final, later, 0)

    slots = [(units - per + part) % SLOTS for part in range(per)]
    fetch_k(units - 1).wait()

    def between():
        fetch_tail(0).wait()
        arrive_all(final - LAG)

    weigh(slots[1], 1, between)
    for g in range(half):
        gather(slots[0], 0, g)
    stats[me, final] = marks[...]
    send_stat(final)
    for n in range(1, 4):
        fetch_tail(n).wait()
        for g in range(half):
            gather(slots[n // 2], n // 2, n % 2 * half + g)
        send_part(final, n - 1, 1, piece_recv.at[n - 1])
    together(final - LAG)
    for b in range(final - LAG + 1, final):
        arrive_all(b)
        together(b)
    arrive(stats, stat_recv.at[final % RING], final)
    shares(final)
    for p in range(pieces):
        arrive(parts, piece_recv.at[p], final, pl.ds(p * PACKED, PACKED))
        combine(final, p)
    arrive(parts, part_send)
    arrive(stats, stat_send)


def solution(mesh):
    ranks = mesh.shape["sp"]

    def step(q, k, v):
        sequences, tokens, kv_heads, head = k.shape
        heads = q.shape[1]
        k, v = (x.transpose(0, 2, 3, 1).reshape(sequences * kv_heads, head, tokens) for x in (k, v))
        hbm = pl.BlockSpec(memory_space=pltpu.HBM)
        dma = pltpu.SemaphoreType.DMA
        return pl.pallas_call(
            functools.partial(kernel, ranks),
            out_shape=jax.ShapeDtypeStruct(q.shape, q.dtype),
            in_specs=[hbm, hbm, hbm],
            out_specs=pl.BlockSpec(memory_space=pltpu.VMEM),
            scratch_shapes=[
                pltpu.VMEM((SLOTS, GROUP, head, tokens), k.dtype),
                pltpu.VMEM((SLOTS, GROUP, head, tokens), v.dtype),
                pltpu.VMEM(q.shape, q.dtype),
                pltpu.VMEM((heads + 8, head), jnp.float32),
                pltpu.VMEM((2, GROUP, 16, tokens), jnp.bfloat16),
                pltpu.VMEM((8, 128), jnp.float32),
                pltpu.VMEM((heads, head), jnp.float32),
                pltpu.VMEM((ranks, sequences, heads // PIECE * PACKED, 128), jnp.bfloat16),
                pltpu.VMEM((ranks, sequences, 8, 128), jnp.float32),
                pltpu.VMEM((ranks, heads, 128), jnp.float32),
                dma((SLOTS,)),
                dma((SLOTS,)),
                dma,
                dma((4,)),
                dma,
                dma((RING,)),
                dma,
                dma((RING,)),
                dma((heads // PIECE,)),
            ],
            compiler_params=pltpu.CompilerParams(collective_id=0, has_side_effects=True, vmem_limit_bytes=42 * 2**20),
        )(pltpu.with_memory_space_constraint(q, pltpu.HBM), k, v)

    return jax.shard_map(
        step,
        mesh=mesh,
        in_specs=(P("dp", None, None), P("dp", "sp", None, None), P("dp", "sp", None, None)),
        out_specs=P("dp", None, None),
        check_vma=False,
    )
```

time: 126 us -> 126 us (level)
  no operation moved by 1% of the time
where the time goes in v4:
time: 126 us
  Pallas kernels  124 us (98%)
    pallas_call x1, Pallas kernels, step(): pl.pallas_call(functools.partial(kernel, ranks), out_shape=jax.ShapeDtype...  124 us

profile of v4, /device:TPU:0, one launch (start us, length us, event | category | flops | bytes accessed | tf_op | source)
XLA Modules:
  0.0 125.6 jit_solution(1390566332601931534)
XLA Ops:
  0.0 124.5 %shard_map.37 = bf16[32,96,192]{2,1,0:T(8,128)(2,1)S(1)} custom-call(bf16[32,96,192]{2,1,0:T(8,128)(2,1)} %q_hbm.1, bf16[256,192,2048]{2,1,0:T(8,128)(2,1)} %bitcast.1.k_hbm, bf16[256,192,2048]{2,1,0:T(8,128)(2,1)} %bitcast.3.v_hbm), custom_call_target="tpu_custom_call" | custom-call | tf_op jit(solution)/shard_map/pallas_call | solution.py:253
  124.5 1.1 copy.5

commit v5 on v4

--- a/solution.py
+++ b/solution.py
@@ -97,10 +97,15 @@
             weights[part, g] = weight.astype(jnp.bfloat16)
         marks[...] = mark
 
+    def weighted(slot, part, g):
+        return lax.dot_general(weights[part, g], values[slot, g], (((1,), (1,)), ((), ())), preferred_element_type=jnp.float32)
+
+    def keep(part, g, result):
+        row = (part * GROUP + g) * each
+        seen[row : row + each] = result[:each]
+
     def gather(slot, part, g):
-        row = (part * GROUP + g) * each
-        result = lax.dot_general(weights[part, g], values[slot, g], (((1,), (1,)), ((), ())), preferred_element_type=jnp.float32)
-        seen[row : row + each] = result[:each]
+        keep(part, g, weighted(slot, part, g))
 
     def pack(b, p):
         rows = seen[p * PIECE : (p + 1) * PIECE]
@@ -223,11 +228,17 @@
         gather(slots[0], 0, g)
     stats[me, final] = marks[...]
     send_stat(final)
-    for n in range(1, 4):
-        fetch_tail(n).wait()
-        for g in range(half):
-            gather(slots[n // 2], n // 2, n % 2 * half + g)
-        send_part(final, n - 1, 1, piece_recv.at[n - 1])
+    held = None
+    for n in range(1, 5):
+        if n < 4:
+            fetch_tail(n).wait()
+            results = [weighted(slots[n // 2], n // 2, n % 2 * half + g) for g in range(half)]
+        if held is not None:
+            m = n - 1
+            for g in range(half):
+                keep(m // 2, m % 2 * half + g, held[g])
+            send_part(final, m - 1, 1, piece_recv.at[m - 1])
+        held = results
     together(final - LAG)
     for b in range(final - LAG + 1, final):
         arrive_all(b)

time: 126 us -> 126 us (level)
  no operation moved by 1% of the time
where the time goes in v5:
time: 126 us
  Pallas kernels  124 us (98%)
    pallas_call x1, Pallas kernels, step(): pl.pallas_call(functools.partial(kernel, ranks), out_shape=jax.ShapeDtype...  124 us

profile of v5, /device:TPU:0, one launch (start us, length us, event | category | flops | bytes accessed | tf_op | source)
XLA Modules:
  0.0 125.5 jit_solution(6530075520455123791)
XLA Ops:
  0.0 124.4 %shard_map.37 = bf16[32,96,192]{2,1,0:T(8,128)(2,1)S(1)} custom-call(bf16[32,96,192]{2,1,0:T(8,128)(2,1)} %q_hbm.1, bf16[256,192,2048]{2,1,0:T(8,128)(2,1)} %bitcast.1.k_hbm, bf16[256,192,2048]{2,1,0:T(8,128)(2,1)} %bitcast.3.v_hbm), custom_call_target="tpu_custom_call" | custom-call | tf_op jit(solution)/shard_map/pallas_call | solution.py:264
  124.4 1.1 copy.5
